TPU v7x, 32 devices: a whole 2x2x4 slice. The times are simulated.
32 devices in a mesh: dp: 8 (over y, x, core), mp: 4 (over z).
Axes of the slice: x: 2, y: 2, z: 4, core: 2. Of those that a mesh axis runs over, the one named last changes fastest.
Arguments:
- layer_in: bfloat16 [16384, 768], P(('dp', 'mp')), may hold values from -6 to 6
- query_proj: bfloat16 [768, 768], P(None, 'mp'), may hold values from -0.21875 to 0.21875
- key_proj: bfloat16 [768, 768], P(None, 'mp'), may hold values from -0.21875 to 0.21875
- value_proj: bfloat16 [768, 768], P(None, 'mp'), may hold values from -0.21875 to 0.21875
- out_proj: bfloat16 [768, 768], P('mp'), may hold values from -1.75 to 1.75
- gate_proj: bfloat16 [768, 2048], P(None, 'mp'), may hold values from -0.21875 to 0.21875
- up_proj: bfloat16 [768, 2048], P(None, 'mp'), may hold values from -0.21875 to 0.21875
- down_proj: bfloat16 [2048, 768], P('mp'), may hold values from -0.125 to 0.125
- first_gain: float32 [768], replicated, may hold values from 0.1 to 1.9
- second_gain: float32 [768], replicated, may hold values from 0.1 to 1.9
- seq_lengths: int32 [16], P('dp'), may hold values from 64 to 1024, as said below
- cotangent: bfloat16 [16384, 768], P(('dp', 'mp')), may hold values from -6 to 6
Outputs:
- layer_out: bfloat16 [16384, 768], P(('dp', 'mp'))
- input_grad: bfloat16 [16384, 768], P(('dp', 'mp'))
- query_grad: float32 [768, 768], P(None, 'mp')
- key_grad: float32 [768, 768], P(None, 'mp')
- value_grad: float32 [768, 768], P(None, 'mp')
- output_grad: float32 [768, 768], P('mp')
- gate_grad: float32 [768, 2048], P(None, 'mp')
- up_grad: float32 [768, 2048], P(None, 'mp')
- down_grad: float32 [2048, 768], P('mp')
- first_grad: float32 [768], replicated
- second_grad: float32 [768], replicated
Inputs may be any that keep to these rules, and one draw needn't show every extreme that they name: Slot i holds a sequence of seq_lengths[i] tokens at its start, the rest of its 1024 rows is padding. Some slot is full in every draw.
All inputs are finite; a program needn't handle non-finite values.
Results may differ from a plain program's by a relative error of at most 0.02.
Values may be sent and summed in bfloat16 or wider, within the bound.
A program may use at most 192 MiB of HBM per device.

v0:
```python
import jax
import jax.numpy as jnp
from jax import lax
from jax.sharding import PartitionSpec as P

HS = 64
SLOT_LEN = 1024


def rms_norm(resid, gain):
    return resid * lax.rsqrt(jnp.mean(resid * resid, axis=-1, keepdims=True) + 1e-05) * gain


def swiglu(gate_pre, up_pre):
    return jax.nn.silu(gate_pre) * up_pre


def rotary_tables(group_rows):
    half = HS // 2
    positions = (jnp.arange(group_rows, dtype=jnp.int32) % SLOT_LEN).astype(jnp.float32)
    freqs = 10000.0 ** (-jnp.arange(half, dtype=jnp.float32) * 2.0 / HS)
    angles = positions[:, None] * freqs[None, :]
    return (jnp.cos(angles)[:, None, :], jnp.sin(angles)[:, None, :])


def rotate(field, cosines, sines):
    half = HS // 2
    first = field[..., :half]
    second = field[..., half:]
    return jnp.concatenate(
        [first * cosines - second * sines, second * cosines + first * sines], axis=-1
    )


def unrotate(grads, cosines, sines):
    half = HS // 2
    first = grads[..., :half]
    second = grads[..., half:]
    return jnp.concatenate(
        [first * cosines + second * sines, second * cosines - first * sines], axis=-1
    )


def cross(left, right):
    return lax.dot_general(
        left, right, (((0,), (0,)), ((), ())), preferred_element_type=jnp.float32
    )


def against(left, right):
    return lax.dot_general(
        left, right, (((1,), (1,)), ((), ())), preferred_element_type=jnp.float32
    )


def block_masks(block_index, block_rows, key_span, valid_len):
    query_pos = block_index * block_rows + jnp.arange(block_rows, dtype=jnp.int32)
    key_pos = jnp.arange(key_span, dtype=jnp.int32)
    allowed = (key_pos[None, :] <= query_pos[:, None]) & (key_pos[None, :] < valid_len)
    present = query_pos < valid_len
    return (allowed, present)


def block_scores(query_block, key_block, allowed):
    scores = (
        jnp.einsum("qhd,khd->hqk", query_block, key_block, preferred_element_type=jnp.float32)
        * 0.125
    )
    return jnp.where(allowed[None], scores, -1e30)


def attend(rot_queries, rot_keys, values_low, seq_lengths):
    block_rows = min(512, SLOT_LEN)
    block_count = SLOT_LEN // block_rows
    mixed_parts = []
    log_norms = []
    for slot_index in range(seq_lengths.shape[0]):
        valid_len = seq_lengths[slot_index]
        base = slot_index * SLOT_LEN
        for block_index in range(block_count):
            start = base + block_index * block_rows
            key_span = (block_index + 1) * block_rows
            allowed, present = block_masks(block_index, block_rows, key_span, valid_len)
            scores = block_scores(
                rot_queries[start : start + block_rows], rot_keys[base : base + key_span], allowed
            )
            top = jnp.max(scores, axis=-1, keepdims=True)
            log_norm = top + jnp.log(jnp.sum(jnp.exp(scores - top), axis=-1, keepdims=True))
            probs_low = jnp.exp(scores - log_norm).astype(jnp.bfloat16)
            mixed = jnp.einsum(
                "hqk,khd->qhd",
                probs_low,
                values_low[base : base + key_span],
                preferred_element_type=jnp.float32,
            )
            mixed_parts.append(mixed * present.astype(jnp.float32)[:, None, None])
            log_norms.append(log_norm)
    return (jnp.concatenate(mixed_parts, axis=0), log_norms)


def attend_back(rot_queries, rot_keys, values_low, d_mixed, log_norms, seq_lengths):
    block_rows = min(512, SLOT_LEN)
    block_count = SLOT_LEN // block_rows
    query_parts = []
    key_parts = []
    value_parts = []
    shape = (SLOT_LEN,) + rot_keys.shape[1:]
    for slot_index in range(seq_lengths.shape[0]):
        valid_len = seq_lengths[slot_index]
        base = slot_index * SLOT_LEN
        key_total = jnp.zeros(shape, jnp.float32)
        value_total = jnp.zeros(shape, jnp.float32)
        for block_index in range(block_count):
            start = base + block_index * block_rows
            key_span = (block_index + 1) * block_rows
            allowed, present = block_masks(block_index, block_rows, key_span, valid_len)
            query_block = rot_queries[start : start + block_rows]
            key_block = rot_keys[base : base + key_span]
            value_block = values_low[base : base + key_span]
            grad_block = (
                d_mixed[start : start + block_rows] * present.astype(jnp.bfloat16)[:, None, None]
            )
            scores = block_scores(query_block, key_block, allowed)
            attn_probs = jnp.exp(scores - log_norms[slot_index * block_count + block_index])
            d_probs = jnp.einsum(
                "qhd,khd->hqk", grad_block, value_block, preferred_element_type=jnp.float32
            )
            d_scores = (
                attn_probs * (d_probs - jnp.sum(d_probs * attn_probs, axis=-1, keepdims=True))
            ).astype(jnp.bfloat16)
            query_parts.append(
                jnp.einsum("hqk,khd->qhd", d_scores, key_block, preferred_element_type=jnp.float32)
                * 0.125
            )
            key_step = (
                jnp.einsum(
                    "hqk,qhd->khd", d_scores, query_block, preferred_element_type=jnp.float32
                )
                * 0.125
            )
            value_step = jnp.einsum(
                "hqk,qhd->khd",
                attn_probs.astype(jnp.bfloat16),
                grad_block,
                preferred_element_type=jnp.float32,
            )
            key_total = key_total.at[:key_span].add(key_step)
            value_total = value_total.at[:key_span].add(value_step)
        key_parts.append(key_total)
        value_parts.append(value_total)
    return (
        jnp.concatenate(query_parts, axis=0),
        jnp.concatenate(key_parts, axis=0),
        jnp.concatenate(value_parts, axis=0),
    )


def body(
    layer_in,
    query_proj,
    key_proj,
    value_proj,
    out_proj,
    gate_proj,
    up_proj,
    down_proj,
    first_gain,
    second_gain,
    seq_lengths,
    cotangent,
):
    head_width = query_proj.shape[1]
    local_heads = head_width // HS
    gathered = lax.all_gather(layer_in, "mp", axis=0, tiled=True)
    group_rows = gathered.shape[0]
    cosines, sines = rotary_tables(group_rows)

    def split_heads(field):
        return field.reshape(group_rows, local_heads, HS)

    rot_queries = rotate(
        split_heads(jnp.dot(gathered, query_proj, preferred_element_type=jnp.float32)),
        cosines,
        sines,
    ).astype(jnp.bfloat16)
    rot_keys = rotate(
        split_heads(jnp.dot(gathered, key_proj, preferred_element_type=jnp.float32)), cosines, sines
    ).astype(jnp.bfloat16)
    values_low = split_heads(
        jnp.dot(gathered, value_proj, preferred_element_type=jnp.float32)
    ).astype(jnp.bfloat16)
    mixed, log_norms = attend(rot_queries, rot_keys, values_low, seq_lengths)
    mixed_low = mixed.reshape(group_rows, head_width).astype(jnp.bfloat16)
    attn_branch = lax.psum_scatter(
        jnp.dot(mixed_low, out_proj, preferred_element_type=jnp.float32).astype(jnp.bfloat16),
        "mp",
        scatter_dimension=0,
        tiled=True,
    ).astype(jnp.float32)
    resid_one = layer_in.astype(jnp.float32) + attn_branch
    normed, first_pull = jax.vjp(rms_norm, resid_one, first_gain)
    normed_all = lax.all_gather(normed.astype(jnp.bfloat16), "mp", axis=0, tiled=True)
    gate_pre = jnp.dot(normed_all, gate_proj, preferred_element_type=jnp.float32)
    up_pre = jnp.dot(normed_all, up_proj, preferred_element_type=jnp.float32)
    hidden = swiglu(gate_pre, up_pre).astype(jnp.bfloat16)
    ffn_branch = lax.psum_scatter(
        jnp.dot(hidden, down_proj, preferred_element_type=jnp.float32).astype(jnp.bfloat16),
        "mp",
        scatter_dimension=0,
        tiled=True,
    ).astype(jnp.float32)
    resid_two = normed + ffn_branch
    result, second_pull = jax.vjp(rms_norm, resid_two, second_gain)
    layer_out = result.astype(jnp.bfloat16)
    d_resid_two, second_part = second_pull(cotangent.astype(jnp.float32))
    ffn_out_all = lax.all_gather(d_resid_two.astype(jnp.bfloat16), "mp", axis=0, tiled=True)
    down_grad = cross(hidden, ffn_out_all)
    d_hidden = against(ffn_out_all, down_proj)
    unused, glu_pull = jax.vjp(swiglu, gate_pre, up_pre)
    d_gate_f, d_up_f = glu_pull(d_hidden)
    d_gate = d_gate_f.astype(jnp.bfloat16)
    d_up = d_up_f.astype(jnp.bfloat16)
    gate_grad = cross(normed_all, d_gate)
    up_grad = cross(normed_all, d_up)
    d_normed = d_resid_two + lax.psum_scatter(
        (against(d_gate, gate_proj) + against(d_up, up_proj)).astype(jnp.bfloat16),
        "mp",
        scatter_dimension=0,
        tiled=True,
    ).astype(jnp.float32)
    d_resid_one, first_part = first_pull(d_normed)
    attn_out_all = lax.all_gather(d_resid_one.astype(jnp.bfloat16), "mp", axis=0, tiled=True)
    output_grad = cross(mixed_low, attn_out_all)
    d_mixed = split_heads(against(attn_out_all, out_proj).astype(jnp.bfloat16))
    d_rot_query, d_rot_key, d_value_raw = attend_back(
        rot_queries, rot_keys, values_low, d_mixed, log_norms, seq_lengths
    )
    d_query = (
        unrotate(d_rot_query, cosines, sines).reshape(group_rows, head_width).astype(jnp.bfloat16)
    )
    d_key = unrotate(d_rot_key, cosines, sines).reshape(group_rows, head_width).astype(jnp.bfloat16)
    d_value = d_value_raw.reshape(group_rows, head_width).astype(jnp.bfloat16)
    query_grad = cross(gathered, d_query)
    key_grad = cross(gathered, d_key)
    value_grad = cross(gathered, d_value)
    input_grad = (
        d_resid_one
        + lax.psum_scatter(
            (
                against(d_query, query_proj)
                + against(d_key, key_proj)
                + against(d_value, value_proj)
            ).astype(jnp.bfloat16),
            "mp",
            scatter_dimension=0,
            tiled=True,
        ).astype(jnp.float32)
    ).astype(jnp.bfloat16)
    query_grad, key_grad, value_grad, output_grad, gate_grad, up_grad, down_grad = lax.psum(
        (query_grad, key_grad, value_grad, output_grad, gate_grad, up_grad, down_grad), "dp"
    )
    first_grad, second_grad = lax.psum((first_part, second_part), ("dp", "mp"))
    return (
        layer_out,
        input_grad,
        query_grad,
        key_grad,
        value_grad,
        output_grad,
        gate_grad,
        up_grad,
        down_grad,
        first_grad,
        second_grad,
    )


def solution(mesh):
    return jax.shard_map(
        body,
        mesh=mesh,
        in_specs=(
            P(("dp", "mp"), None),
            P(None, "mp"),
            P(None, "mp"),
            P(None, "mp"),
            P("mp", None),
            P(None, "mp"),
            P(None, "mp"),
            P("mp", None),
            P(),
            P(),
            P("dp"),
            P(("dp", "mp"), None),
        ),
        out_specs=(
            P(("dp", "mp"), None),
            P(("dp", "mp"), None),
            P(None, "mp"),
            P(None, "mp"),
            P(None, "mp"),
            P("mp", None),
            P(None, "mp"),
            P(None, "mp"),
            P("mp", None),
            P(),
            P(),
        ),
        check_vma=False,
    )
```

profile of v0, /device:TPU:0, one launch (start us, length us, event | category | flops | bytes accessed | tf_op | source)
XLA Modules:
  0.0 745.8 jit_solution(7970744030019012255)
XLA Ops:
  21.5 54.3 %all-gather.5.cloned.1.call-done = bf16[2048,768]{1,0:T(8,128)(2,1)} async-done(((bf16[512,768]{1,0:T(8,128)(2,1)}), bf16[2048,768]{1,0:T(8,128)(2,1)}) %all-gather.5.cloned.1.call-update) | async-done | bytes 3145744 | tf_op jit(solution)/shard_map/all_gather | solution.py:174
  75.8 3.2 convolution_convert_fusion.3
  88.0 3.7 exponential_reduce_fusion
  98.9 2.7 convolution_convert_fusion.1
  101.7 59.1 %reduce-scatter.5.cloned.1.call-done = bf16[512,768]{1,0:T(8,128)(2,1)} async-done(((bf16[2048,768]{1,0:T(8,128)(2,1)}), bf16[512,768]{1,0:T(8,128)(2,1)}) %reduce-scatter.5.cloned.1.call-update) | async-done | bytes 786448 | tf_op jit(solution)/shard_map/reduce_scatter | solution.py:194
  162.9 2.3 multiply_convert_fusion.7
  165.3 63.5 %all-gather.7.cloned.1.call-done = bf16[2048,768]{1,0:T(8,128)(2,1)} async-done(((bf16[512,768]{1,0:T(8,128)(2,1)}), bf16[2048,768]{1,0:T(8,128)(2,1)}) %all-gather.7.cloned.1.call-update) | async-done | bytes 3145744 | tf_op jit(solution)/shard_map/all_gather | solution.py:202
  228.8 3.8 fusion.119
  232.7 4.3 multiply_convert_fusion.3
  238.3 3.4 convolution_convert_fusion
  242.2 58.8 %reduce-scatter.7.cloned.1.call-done = bf16[512,768]{1,0:T(8,128)(2,1)} async-done(((bf16[2048,768]{1,0:T(8,128)(2,1)}), bf16[512,768]{1,0:T(8,128)(2,1)}) %reduce-scatter.7.cloned.1.call-update) | async-done | bytes 786448 | tf_op jit(solution)/shard_map/reduce_scatter | solution.py:206
  304.0 2.2 fusion.112
  306.3 63.5 %all-gather.9.cloned.1.call-done = bf16[2048,768]{1,0:T(8,128)(2,1)} async-done(((bf16[512,768]{1,0:T(8,128)(2,1)}), bf16[2048,768]{1,0:T(8,128)(2,1)}) %all-gather.9.cloned.1.call-update) | async-done | bytes 3145744 | tf_op jit(solution)/shard_map/all_gather | solution.py:216
  369.7 6.3 multiply_convert_fusion.2
  377.9 3.5 add_convert_fusion.1
  381.5 59.2 %reduce-scatter.9.cloned.1.call-done = bf16[512,768]{1,0:T(8,128)(2,1)} async-done(((bf16[2048,768]{1,0:T(8,128)(2,1)}), bf16[512,768]{1,0:T(8,128)(2,1)}) %reduce-scatter.9.cloned.1.call-update) | async-done | bytes 786448 | tf_op jit(solution)/shard_map/reduce_scatter | solution.py:225
  440.7 3.0 multiply_reduce_fusion.4
  446.7 63.2 %all-gather.11.cloned.1.call-done = bf16[2048,768]{1,0:T(8,128)(2,1)} async-done(((bf16[512,768]{1,0:T(8,128)(2,1)}), bf16[2048,768]{1,0:T(8,128)(2,1)}) %all-gather.11.cloned.1.call-update) | async-done | bytes 3145744 | tf_op jit(solution)/shard_map/all_gather | solution.py:232
  510.0 3.1 convolution_convert_fusion.2
  513.2 3.0 convolution_bitcast_fusion.5
  524.7 2.5 multiply_reduce_fusion.1
  527.3 2.6 fusion.25
  529.9 2.7 multiply_reduce_fusion
  532.6 2.6 fusion.24
  547.9 2.9 add_convert_fusion
  551.1 5.7 fusion.126
  556.8 3.0 fusion.125
  559.8 3.0 fusion.124
  570.6 43.9 %all-reduce.4 = (f32[768]{0:T(1024)}, f32[768]{0:T(1024)}) all-reduce(f32[768]{0:T(1024)S(1)} %copy-done.80, f32[768]{0:T(1024)S(1)} %copy-done.79), channel_id=1, replica_groups=mesh['dp'=8,'mp'=4] {'dp','mp'}, use_global_device_ids=true, to_apply=%region_28.29 | all-reduce | flops 1536 | bytes 12288 | tf_op jit(solution)/shard_map/psum | solution.py:262
  614.5 3.2 add_convert_fusion.2
  617.7 110.9 %all-reduce.8.cloned.1.call-done = (f32[768,192]{0,1:T(8,128)}, f32[768,192]{0,1:T(8,128)}, f32[768,192]{0,1:T(8,128)}, f32[192,768]{1,0:T(8,128)}, f32[768,512]...) async-done(((f32[768,192]{0,1:T(8,128)}, f32[768,192]{0,1:T(8,128)}, f32[768,192]{0,1:T(8,128)}, f32[192,768]{1,0:T(8,128)}, f32[768,512]{1,0:T(8,128)}, ...) | async-done | bytes 7077904 | tf_op jit(solution)/shard_map/psum | solution.py:259
  728.6 2.1 copy.46
  (292 shorter events, 79.3 us)
Async XLA Ops:
  7.2 231.1 %copy-start = (bf16[512,768]{1,0:T(8,128)(2,1)S(1)}, bf16[512,768]{1,0:T(8,128)(2,1)}, u32[]{:S(2)}) copy-start(bf16[512,768]{1,0:T(8,128)(2,1)} %param.43) | copy-start | bytes 2359300
  7.2 68.6 %all-gather.5.cloned.1.call-start = ((), (), s32[]{:S(2)}) async-start(), calls=%async_computation.4 | async-start | bytes 3932160 | tf_op jit(solution)/shard_map/all_gather | solution.py:174
  7.9 152.9 %reduce-scatter.5.cloned.1.call-start = ((), (), s32[]{:S(2)}) async-start(), calls=%async_computation.5 | async-start | bytes 3932160 | tf_op jit(solution)/shard_map/reduce_scatter | solution.py:194
  18.2 74.7 %copy-start.35 = (pred[512,512]{0,1:T(8,128)(4,1)}, pred[512,512]{0,1:T(8,128)(4,1)S(1)}, u32[]{:S(2)}) copy-start(pred[512,512]{0,1:T(8,128)(4,1)S(1)} %fusion.40) | copy-start | bytes 786436
  18.3 73.4 %copy-start.33 = (pred[512,512]{0,1:T(8,128)(4,1)}, pred[512,512]{0,1:T(8,128)(4,1)S(1)}, u32[]{:S(2)}) copy-start(pred[512,512]{0,1:T(8,128)(4,1)S(1)} %fusion.41) | copy-start | bytes 786436
  19.7 76.2 %copy-start.15 = (pred[512,1024]{1,0:T(8,128)(4,1)}, pred[512,1024]{1,0:T(8,128)(4,1)S(1)}, u32[]{:S(2)}) copy-start(pred[512,1024]{1,0:T(8,128)(4,1)S(1)} %get-tuple-element.182) | copy-start | bytes 1572868
  21.5 57.6 %copy-start.54 = (bf16[768,192]{0,1:T(8,128)(2,1)S(1)}, bf16[768,192]{0,1:T(8,128)(2,1)}, u32[]{:S(2)}) copy-start(bf16[768,192]{0,1:T(8,128)(2,1)} %param.38) | copy-start | bytes 884740
  79.0 12.7 %copy-start.56 = (bf16[512,192]{0,1:T(8,128)(2,1)}, bf16[512,192]{0,1:T(8,128)(2,1)S(1)}, u32[]{:S(2)}) copy-start(bf16[512,192]{0,1:T(8,128)(2,1)S(1)} %get-tuple-element.171) | copy-start | bytes 589828
  79.0 13.8 %copy-start.58 = (bf16[512,192]{0,1:T(8,128)(2,1)}, bf16[512,192]{0,1:T(8,128)(2,1)S(1)}, u32[]{:S(2)}) copy-start(bf16[512,192]{0,1:T(8,128)(2,1)S(1)} %get-tuple-element.172) | copy-start | bytes 589828
  79.1 14.7 %copy-start.47 = (bf16[1024,192]{0,1:T(8,128)(2,1)}, bf16[1024,192]{0,1:T(8,128)(2,1)S(1)}, u32[]{:S(2)}) copy-start(bf16[1024,192]{0,1:T(8,128)(2,1)S(1)} %get-tuple-element.173) | copy-start | bytes 1179652
  79.1 16.7 %copy-start.45 = (bf16[1024,192]{0,1:T(8,128)(2,1)}, bf16[1024,192]{0,1:T(8,128)(2,1)S(1)}, u32[]{:S(2)}) copy-start(bf16[1024,192]{0,1:T(8,128)(2,1)S(1)} %get-tuple-element.174) | copy-start | bytes 1179652
  82.9 8.9 %copy-start.6 = (f32[3,512,512]{1,2,0:T(8,128)}, f32[3,512,512]{1,2,0:T(8,128)S(1)}, u32[]{:S(2)}) copy-start(f32[3,512,512]{1,2,0:T(8,128)S(1)} %get-tuple-element.192) | copy-start | bytes 9437188
  83.6 8.2 %copy-start.72 = (f32[3,512]{1,0:T(4,128)}, f32[3,512]{1,0:T(4,128)S(1)}, u32[]{:S(2)}) copy-start(f32[3,512]{1,0:T(4,128)S(1)} %log_add_fusion.3) | copy-start | bytes 18436
  84.4 8.4 %copy-start.8 = (f32[3,512,512]{1,2,0:T(8,128)}, f32[3,512,512]{1,2,0:T(8,128)S(1)}, u32[]{:S(2)}) copy-start(f32[3,512,512]{1,2,0:T(8,128)S(1)} %get-tuple-element.188) | copy-start | bytes 9437188
  85.2 7.7 %copy-start.74 = (f32[3,512]{1,0:T(4,128)}, f32[3,512]{1,0:T(4,128)S(1)}, u32[]{:S(2)}) copy-start(f32[3,512]{1,0:T(4,128)S(1)} %log_add_fusion.1) | copy-start | bytes 18436
  88.0 7.9 %copy-start.4 = (f32[3,512,1024]{2,1,0:T(8,128)}, f32[3,512,1024]{2,1,0:T(8,128)S(1)}, u32[]{:S(2)}) copy-start(f32[3,512,1024]{2,1,0:T(8,128)S(1)} %get-tuple-element.186) | copy-start | bytes 18874372
  101.6 59.2 %copy-start.10 = (bf16[512,768]{1,0:T(8,128)(2,1)S(1)}, bf16[512,768]{1,0:T(8,128)(2,1)}, u32[]{:S(2)}) copy-start(bf16[512,768]{1,0:T(8,128)(2,1)} %param.36) | copy-start | bytes 2359300
  101.6 61.3 %copy-start.69 = (f32[768]{0:T(1024)S(1)}, f32[768]{0:T(1024)}, u32[]{:S(2)}) copy-start(f32[768]{0:T(1024)} %param.44) | copy-start | bytes 9220
  101.7 127.1 %copy-start.60 = (bf16[768,512]{1,0:T(8,128)(2,1)S(1)}, bf16[768,512]{1,0:T(8,128)(2,1)}, u32[]{:S(2)}) copy-start(bf16[768,512]{1,0:T(8,128)(2,1)} %param.41) | copy-start | bytes 2359300
  101.7 127.1 %all-gather.7.cloned.1.call-start = ((), (), s32[]{:S(2)}) async-start(), calls=%async_computation.6 | async-start | bytes 3932160 | tf_op jit(solution)/shard_map/all_gather | solution.py:202
  165.3 135.7 %reduce-scatter.7.cloned.1.call-start = ((), (), s32[]{:S(2)}) async-start(), calls=%async_computation.7 | async-start | bytes 3932160 | tf_op jit(solution)/shard_map/reduce_scatter | solution.py:206
  241.7 59.2 %copy-start.11 = (bf16[512,768]{1,0:T(8,128)(2,1)S(1)}, bf16[512,768]{1,0:T(8,128)(2,1)}, u32[]{:S(2)}) copy-start(bf16[512,768]{1,0:T(8,128)(2,1)} %reduce-scatter.5.cloned.1.call-done) | copy-start | bytes 2359300
  241.8 127.9 %all-gather.9.cloned.1.call-start = ((), (), s32[]{:S(2)}) async-start(), calls=%async_computation.8 | async-start | bytes 3932160 | tf_op jit(solution)/shard_map/all_gather | solution.py:216
  306.2 134.5 %reduce-scatter.9.cloned.1.call-start = ((), (), s32[]{:S(2)}) async-start(), calls=%async_computation.9 | async-start | bytes 3932160 | tf_op jit(solution)/shard_map/reduce_scatter | solution.py:225
  381.5 128.5 %all-gather.11.cloned.1.call-start = ((), (), s32[]{:S(2)}) async-start(), calls=%async_computation.10 | async-start | bytes 3932160 | tf_op jit(solution)/shard_map/all_gather | solution.py:232
  446.5 66.7 %copy-start.36 = (pred[512,512]{0,1:T(8,128)(4,1)S(1)}, pred[512,512]{0,1:T(8,128)(4,1)}, u32[]{:S(2)}) copy-start(pred[512,512]{0,1:T(8,128)(4,1)} %copy-done.35) | copy-start | bytes 786436
  446.5 66.7 %copy-start.75 = (f32[3,512]{1,0:T(4,128)S(1)}, f32[3,512]{1,0:T(4,128)}, u32[]{:S(2)}) copy-start(f32[3,512]{1,0:T(4,128)} %copy-done.74) | copy-start | bytes 18436
  446.5 66.7 %copy-start.83 = (bf16[512]{0:T(512)(128)(2,1)S(1)}, bf16[512]{0:T(512)(128)(2,1)}, u32[]{:S(2)}) copy-start(bf16[512]{0:T(512)(128)(2,1)} %get-tuple-element.206) | copy-start | bytes 3076
  446.5 168.0 %reduce-scatter.11.cloned.1.call-start = ((), (), s32[]{:S(2)}) async-start(), calls=%async_computation.11 | async-start | bytes 3932160 | tf_op jit(solution)/shard_map/reduce_scatter | solution.py:248
  550.8 177.8 %all-reduce.8.cloned.1.call-start = ((), (), s32[]{:S(2)}) async-start(), calls=%async_computation.12 | async-start | bytes 14155776 | tf_op jit(solution)/shard_map/psum | solution.py:259
  569.9 44.6 %copy-start.32 = (bf16[512,768]{1,0:T(8,128)(2,1)S(1)}, bf16[512,768]{1,0:T(8,128)(2,1)}, u32[]{:S(2)}) copy-start(bf16[512,768]{1,0:T(8,128)(2,1)} %reduce-scatter.9.cloned.1.call-done) | copy-start | bytes 2359300
  569.9 44.6 %copy-start.77 = (f32[512]{0:T(512)S(1)}, f32[512]{0:T(512)}, u32[]{:S(2)}) copy-start(f32[512]{0:T(512)} %copy-done.76) | copy-start | bytes 6148
  (73 other events, 190.4 us)
Sparse Core Ops, SparseCore 0:
  9.6 66.1 all-gather.4
  101.8 59.0 reduce-scatter.4
  165.4 63.3 all-gather.6
  241.9 59.0 reduce-scatter.6
  306.3 63.3 all-gather.8
  381.6 59.0 reduce-scatter.8
  446.6 63.3 all-gather.10
  550.9 60.1 reduce-scatter.10
  615.9 112.6 all-reduce.7
where the time goes:
time: 755 us; the launch traced here: 746 us
  waiting for transfers between devices  533 us (71%)
  matrix products  90 us (12%)
  blocking collectives  43.9 us (6%)
  other arithmetic  41.5 us (5%)
  local copies, waits for them, and re-layouts  20.5 us (3%)
  between operations  15.5 us (2%)
    psum x1, waiting for transfers between devices, body(): lax.psum((query_grad, key_grad, value_grad, output_grad, gate_grad, up_gr...  111 us
    all_gather x1, waiting for transfers between devices, body(): lax.all_gather(normed.astype(jnp.bfloat16), 'mp', axis=0, tiled=True)  63.5 us
    all_gather x1, waiting for transfers between devices, body(): lax.all_gather(d_resid_two.astype(jnp.bfloat16), 'mp', axis=0, tiled=True)  63.5 us
    all_gather x1, waiting for transfers between devices, body(): lax.all_gather(d_resid_one.astype(jnp.bfloat16), 'mp', axis=0, tiled=True)  63.2 us
    reduce_scatter x1, waiting for transfers between devices, body(): lax.psum_scatter((against(d_gate, gate_proj) + against(d_up, up_proj)).as...  59.2 us
    reduce_scatter x1, waiting for transfers between devices, body(): lax.psum_scatter(jnp.dot(mixed_low, out_proj, preferred_element_type=jnp....  59.1 us
    reduce_scatter x1, waiting for transfers between devices, body(): lax.psum_scatter(jnp.dot(hidden, down_proj, preferred_element_type=jnp.fl...  58.8 us
    all_gather x1, waiting for transfers between devices, body(): gathered = lax.all_gather(layer_in, 'mp', axis=0, tiled=True)  54.3 us
  transfers between devices with their start and end apart: 9, of which 8 were waited for; matrix products, arithmetic and copies ran while one was open for 5% of the time, Pallas kernels for 0%

commit v1 on v0

--- a/solution.py
+++ b/solution.py
@@ -5,6 +5,18 @@
 
 HS = 64
 SLOT_LEN = 1024
+
+
+def gather_by_bits(array, axis, dim):
+    ways, here = (lax.axis_size(axis), lax.axis_index(axis))
+    grown, reach = (array, 1)
+    while reach < ways:
+        theirs = lax.ppermute(grown, axis, [(d, d ^ reach) for d in range(ways)])
+        mine_first = jnp.concatenate([grown, theirs], axis=dim)
+        theirs_first = jnp.concatenate([theirs, grown], axis=dim)
+        grown = jnp.where(here & reach == 0, mine_first, theirs_first)
+        reach = 2 * reach
+    return grown
 
 
 def rms_norm(resid, gain):
@@ -213,7 +225,7 @@
     result, second_pull = jax.vjp(rms_norm, resid_two, second_gain)
     layer_out = result.astype(jnp.bfloat16)
     d_resid_two, second_part = second_pull(cotangent.astype(jnp.float32))
-    ffn_out_all = lax.all_gather(d_resid_two.astype(jnp.bfloat16), "mp", axis=0, tiled=True)
+    ffn_out_all = gather_by_bits(d_resid_two.astype(jnp.bfloat16), "mp", 0)
     down_grad = cross(hidden, ffn_out_all)
     d_hidden = against(ffn_out_all, down_proj)
     unused, glu_pull = jax.vjp(swiglu, gate_pre, up_pre)

time: 755 us -> 789 us (1.045)
  waiting for transfers between devices: 533 us -> 556 us
    ppermute x0 -> x2, waiting for transfers between devices: none -> 85.8 us  [gather_by_bits(): theirs = lax.ppermute(grown, axis, [(d, d ^ reach) for d in range(ways)])]
    all_gather x1 -> x0, waiting for transfers between devices: 63.5 us -> none  [body(): lax.all_gather(d_resid_two.astype(jnp.bfloat16), 'mp', axis=0, tiled=True)]
  transfers between devices with their start and end apart: 9 -> 10, of which waited for: 8 -> 9; matrix products, arithmetic and copies ran while one was open for 5% -> 5% of each run, Pallas kernels for 0% -> 0%
where the time goes in v1:
time: 789 us; the launch traced here: 780 us
  waiting for transfers between devices  556 us (70%)
  matrix products  96.1 us (12%)
  other arithmetic  45.1 us (6%)
  blocking collectives  42 us (5%)
  local copies, waits for them, and re-layouts  20.7 us (3%)
  between operations  15.8 us (2%)
    psum x1, waiting for transfers between devices, body(): lax.psum((query_grad, key_grad, value_grad, output_grad, gate_grad, up_gr...  110 us
    ppermute x2, waiting for transfers between devices, gather_by_bits(): theirs = lax.ppermute(grown, axis, [(d, d ^ reach) for d in range(ways)])  85.8 us
    all_gather x1, waiting for transfers between devices, body(): lax.all_gather(normed.astype(jnp.bfloat16), 'mp', axis=0, tiled=True)  63.5 us
    all_gather x1, waiting for transfers between devices, body(): lax.all_gather(d_resid_one.astype(jnp.bfloat16), 'mp', axis=0, tiled=True)  63.3 us
    reduce_scatter x1, waiting for transfers between devices, body(): lax.psum_scatter((against(d_gate, gate_proj) + against(d_up, up_proj)).as...  60.6 us
    reduce_scatter x1, waiting for transfers between devices, body(): lax.psum_scatter(jnp.dot(mixed_low, out_proj, preferred_element_type=jnp....  59.1 us
    reduce_scatter x1, waiting for transfers between devices, body(): lax.psum_scatter(jnp.dot(hidden, down_proj, preferred_element_type=jnp.fl...  58.8 us
    all_gather x1, waiting for transfers between devices, body(): gathered = lax.all_gather(layer_in, 'mp', axis=0, tiled=True)  54.3 us
  transfers between devices with their start and end apart: 10, of which 9 were waited for; matrix products, arithmetic and copies ran while one was open for 5% of the time, Pallas kernels for 0%

profile of v1, /device:TPU:0, one launch (start us, length us, event | category | flops | bytes accessed | tf_op | source)
XLA Modules:
  0.0 780.0 jit_solution(4919859925644502734)
XLA Ops:
  21.5 54.3 %all-gather.4.cloned.1.call-done = bf16[2048,768]{1,0:T(8,128)(2,1)} async-done(((bf16[512,768]{1,0:T(8,128)(2,1)}), bf16[2048,768]{1,0:T(8,128)(2,1)}) %all-gather.4.cloned.1.call-update) | async-done | bytes 3145744 | tf_op jit(solution)/shard_map/all_gather | solution.py:186
  75.8 3.2 convolution_convert_fusion.3
  88.0 3.7 exponential_reduce_fusion
  98.9 2.8 convolution_convert_fusion.1
  101.8 59.1 %reduce-scatter.5.cloned.1.call-done = bf16[512,768]{1,0:T(8,128)(2,1)} async-done(((bf16[2048,768]{1,0:T(8,128)(2,1)}), bf16[512,768]{1,0:T(8,128)(2,1)}) %reduce-scatter.5.cloned.1.call-update) | async-done | bytes 786448 | tf_op jit(solution)/shard_map/reduce_scatter | solution.py:206
  165.4 63.5 %all-gather.6.cloned.1.call-done = bf16[2048,768]{1,0:T(8,128)(2,1)} async-done(((bf16[512,768]{1,0:T(8,128)(2,1)}), bf16[2048,768]{1,0:T(8,128)(2,1)}) %all-gather.6.cloned.1.call-update) | async-done | bytes 3145744 | tf_op jit(solution)/shard_map/all_gather | solution.py:214
  228.8 3.8 fusion.123
  232.7 4.3 multiply_convert_fusion.3
  238.4 3.5 convolution_convert_fusion
  242.4 58.8 %reduce-scatter.7.cloned.1.call-done = bf16[512,768]{1,0:T(8,128)(2,1)} async-done(((bf16[2048,768]{1,0:T(8,128)(2,1)}), bf16[512,768]{1,0:T(8,128)(2,1)}) %reduce-scatter.7.cloned.1.call-update) | async-done | bytes 786448 | tf_op jit(solution)/shard_map/reduce_scatter | solution.py:218
  307.2 18.3 %collective-permute-done = bf16[512,768]{1,0:T(8,128)(2,1)} collective-permute-done((bf16[512,768]{1,0:T(8,128)(2,1)}, bf16[512,768]{1,0:T(8,128)(2,1)}, u32[]{:S(2)}, u32[]{:S(2)}) %collective-permute-start) | collective-permute-done | bytes 786464 | tf_op jit(solution)/shard_map/ppermute | solution.py:14
  325.5 3.6 maximum_select_fusion.1
  329.1 2.7 collective-permute-start.1
  331.8 67.5 %collective-permute-done.1 = bf16[1024,768]{1,0:T(8,128)(2,1)} collective-permute-done((bf16[1024,768]{1,0:T(8,128)(2,1)}, bf16[1024,768]{1,0:T(8,128)(2,1)}, u32[]{:S(2)}, u32[]{:S(2)}) %collective-permute-start.1) | collective-permute-done | bytes 1572896 | tf_op jit(solution)/shard_map/ppermute | solution.py:14
  399.3 9.0 %multiply_convert_fusion.2 = (bf16[2048,512]{1,0:T(8,128)(2,1)S(1)}, bf16[2048,512]{1,0:T(8,128)(2,1)S(1)}) fusion(f32[2048,512]{1,0:T(8,128)} %copy-done.89, f32[2048,512]{1,0:T(8,128)} %get-tuple-element.194, bf16[512,768]{1,0:T(8,128)(2,1)S(1)} %copy-done, bf16[1024,768]{1,0:T(8,128)(2,1)} %collective-permute-done.1, ...), kind=kOutput, calls=%fused_computation.18 | convolution fusion | flops 1639448576 | bytes 16515073 | tf_op jit(solution)/shard_map/dot_general | solution.py:63
  410.4 3.6 add_convert_fusion.1
  414.0 60.6 %reduce-scatter.9.cloned.1.call-done = bf16[512,768]{1,0:T(8,128)(2,1)} async-done(((bf16[2048,768]{1,0:T(8,128)(2,1)}), bf16[512,768]{1,0:T(8,128)(2,1)}) %reduce-scatter.9.cloned.1.call-update) | async-done | bytes 786448 | tf_op jit(solution)/shard_map/reduce_scatter | solution.py:237
  474.6 3.0 multiply_reduce_fusion.4
  480.7 63.3 %all-gather.8.cloned.1.call-done = bf16[2048,768]{1,0:T(8,128)(2,1)} async-done(((bf16[512,768]{1,0:T(8,128)(2,1)}), bf16[2048,768]{1,0:T(8,128)(2,1)}) %all-gather.8.cloned.1.call-update) | async-done | bytes 3145744 | tf_op jit(solution)/shard_map/all_gather | solution.py:244
  543.9 3.1 convolution_convert_fusion.2
  547.1 3.0 convolution_bitcast_fusion.5
  558.7 2.5 multiply_reduce_fusion.1
  561.2 2.6 fusion.25
  563.9 2.7 multiply_reduce_fusion
  566.6 2.6 fusion.24
  581.9 2.8 add_convert_fusion
  585.0 5.7 fusion.129
  590.8 3.0 fusion.128
  593.8 6.2 fusion.43
  607.8 42.0 %all-reduce.4 = (f32[768]{0:T(1024)}, f32[768]{0:T(1024)}) all-reduce(f32[768]{0:T(1024)S(1)} %copy-done.79, f32[768]{0:T(1024)S(1)} %copy-done.78), channel_id=1, replica_groups=mesh['dp'=8,'mp'=4] {'dp','mp'}, use_global_device_ids=true, to_apply=%region_28.29 | all-reduce | flops 1536 | bytes 12288 | tf_op jit(solution)/shard_map/psum | solution.py:274
  649.7 3.2 add_convert_fusion.2
  652.9 109.5 %all-reduce.8.cloned.1.call-done = (f32[768,192]{0,1:T(8,128)}, f32[768,192]{0,1:T(8,128)}, f32[768,192]{0,1:T(8,128)}, f32[192,768]{1,0:T(8,128)}, f32[768,512]...) async-done(((f32[768,192]{0,1:T(8,128)}, f32[768,192]{0,1:T(8,128)}, f32[768,192]{0,1:T(8,128)}, f32[192,768]{1,0:T(8,128)}, f32[768,512]{1,0:T(8,128)}, ...) | async-done | bytes 7077904 | tf_op jit(solution)/shard_map/psum | solution.py:271
  (294 shorter events, 86.8 us)
Async XLA Ops:
  7.2 231.2 %copy-start = (bf16[512,768]{1,0:T(8,128)(2,1)S(1)}, bf16[512,768]{1,0:T(8,128)(2,1)}, u32[]{:S(2)}) copy-start(bf16[512,768]{1,0:T(8,128)(2,1)} %param.43) | copy-start | bytes 2359300
  7.2 68.6 %all-gather.4.cloned.1.call-start = ((), (), s32[]{:S(2)}) async-start(), calls=%async_computation.4 | async-start | bytes 3932160 | tf_op jit(solution)/shard_map/all_gather | solution.py:186
  7.9 153.0 %reduce-scatter.5.cloned.1.call-start = ((), (), s32[]{:S(2)}) async-start(), calls=%async_computation.5 | async-start | bytes 3932160 | tf_op jit(solution)/shard_map/reduce_scatter | solution.py:206
  18.1 74.7 %copy-start.34 = (pred[512,512]{0,1:T(8,128)(4,1)}, pred[512,512]{0,1:T(8,128)(4,1)S(1)}, u32[]{:S(2)}) copy-start(pred[512,512]{0,1:T(8,128)(4,1)S(1)} %fusion.40) | copy-start | bytes 786436
  18.3 73.5 %copy-start.32 = (pred[512,512]{0,1:T(8,128)(4,1)}, pred[512,512]{0,1:T(8,128)(4,1)S(1)}, u32[]{:S(2)}) copy-start(pred[512,512]{0,1:T(8,128)(4,1)S(1)} %fusion.41) | copy-start | bytes 786436
  19.7 76.2 %copy-start.15 = (pred[512,1024]{1,0:T(8,128)(4,1)}, pred[512,1024]{1,0:T(8,128)(4,1)S(1)}, u32[]{:S(2)}) copy-start(pred[512,1024]{1,0:T(8,128)(4,1)S(1)} %get-tuple-element.182) | copy-start | bytes 1572868
  21.5 57.6 %copy-start.53 = (bf16[768,192]{0,1:T(8,128)(2,1)S(1)}, bf16[768,192]{0,1:T(8,128)(2,1)}, u32[]{:S(2)}) copy-start(bf16[768,192]{0,1:T(8,128)(2,1)} %param.38) | copy-start | bytes 884740
  79.0 12.7 %copy-start.55 = (bf16[512,192]{0,1:T(8,128)(2,1)}, bf16[512,192]{0,1:T(8,128)(2,1)S(1)}, u32[]{:S(2)}) copy-start(bf16[512,192]{0,1:T(8,128)(2,1)S(1)} %get-tuple-element.171) | copy-start | bytes 589828
  79.0 13.8 %copy-start.57 = (bf16[512,192]{0,1:T(8,128)(2,1)}, bf16[512,192]{0,1:T(8,128)(2,1)S(1)}, u32[]{:S(2)}) copy-start(bf16[512,192]{0,1:T(8,128)(2,1)S(1)} %get-tuple-element.172) | copy-start | bytes 589828
  79.1 14.7 %copy-start.46 = (bf16[1024,192]{0,1:T(8,128)(2,1)}, bf16[1024,192]{0,1:T(8,128)(2,1)S(1)}, u32[]{:S(2)}) copy-start(bf16[1024,192]{0,1:T(8,128)(2,1)S(1)} %get-tuple-element.173) | copy-start | bytes 1179652
  79.1 16.7 %copy-start.44 = (bf16[1024,192]{0,1:T(8,128)(2,1)}, bf16[1024,192]{0,1:T(8,128)(2,1)S(1)}, u32[]{:S(2)}) copy-start(bf16[1024,192]{0,1:T(8,128)(2,1)S(1)} %get-tuple-element.174) | copy-start | bytes 1179652
  82.9 8.9 %copy-start.6 = (f32[3,512,512]{1,2,0:T(8,128)}, f32[3,512,512]{1,2,0:T(8,128)S(1)}, u32[]{:S(2)}) copy-start(f32[3,512,512]{1,2,0:T(8,128)S(1)} %get-tuple-element.192) | copy-start | bytes 9437188
  83.6 8.2 %copy-start.71 = (f32[3,512]{1,0:T(4,128)}, f32[3,512]{1,0:T(4,128)S(1)}, u32[]{:S(2)}) copy-start(f32[3,512]{1,0:T(4,128)S(1)} %log_add_fusion.3) | copy-start | bytes 18436
  84.4 8.4 %copy-start.8 = (f32[3,512,512]{1,2,0:T(8,128)}, f32[3,512,512]{1,2,0:T(8,128)S(1)}, u32[]{:S(2)}) copy-start(f32[3,512,512]{1,2,0:T(8,128)S(1)} %get-tuple-element.188) | copy-start | bytes 9437188
  101.7 59.2 %copy-start.10 = (bf16[512,768]{1,0:T(8,128)(2,1)S(1)}, bf16[512,768]{1,0:T(8,128)(2,1)}, u32[]{:S(2)}) copy-start(bf16[512,768]{1,0:T(8,128)(2,1)} %param.36) | copy-start | bytes 2359300
  101.7 61.3 %copy-start.68 = (f32[768]{0:T(1024)S(1)}, f32[768]{0:T(1024)}, u32[]{:S(2)}) copy-start(f32[768]{0:T(1024)} %param.44) | copy-start | bytes 9220
  101.7 127.1 %copy-start.59 = (bf16[768,512]{1,0:T(8,128)(2,1)S(1)}, bf16[768,512]{1,0:T(8,128)(2,1)}, u32[]{:S(2)}) copy-start(bf16[768,512]{1,0:T(8,128)(2,1)} %param.41) | copy-start | bytes 2359300
  101.7 127.1 %all-gather.6.cloned.1.call-start = ((), (), s32[]{:S(2)}) async-start(), calls=%async_computation.6 | async-start | bytes 3932160 | tf_op jit(solution)/shard_map/all_gather | solution.py:214
  165.3 135.8 %reduce-scatter.7.cloned.1.call-start = ((), (), s32[]{:S(2)}) async-start(), calls=%async_computation.7 | async-start | bytes 3932160 | tf_op jit(solution)/shard_map/reduce_scatter | solution.py:218
  241.9 59.2 %copy-start.11 = (bf16[512,768]{1,0:T(8,128)(2,1)S(1)}, bf16[512,768]{1,0:T(8,128)(2,1)}, u32[]{:S(2)}) copy-start(bf16[512,768]{1,0:T(8,128)(2,1)} %reduce-scatter.5.cloned.1.call-done) | copy-start | bytes 2359300
  241.9 232.7 %reduce-scatter.9.cloned.1.call-start = ((), (), s32[]{:S(2)}) async-start(), calls=%async_computation.8 | async-start | bytes 3932160 | tf_op jit(solution)/shard_map/reduce_scatter | solution.py:237
  306.3 19.2 %collective-permute-start = (bf16[512,768]{1,0:T(8,128)(2,1)}, bf16[512,768]{1,0:T(8,128)(2,1)}, u32[]{:S(2)}, u32[]{:S(2)}) collective-permute-start(bf16[512,768]{1,0:T(8,128)(2,1)} %get-tuple-element.152), channel_id=1, source_target_pairs={{0,1},{1,0},{2,3},{3,2},{4,5},{5,4},{6,7},{7,6},{8,9},{9,8},{10,11... | collective-permute-start | bytes 2359304 | tf_op jit(solution)/shard_map/ppermute | solution.py:14
  329.1 70.2 %collective-permute-start.1 = (bf16[1024,768]{1,0:T(8,128)(2,1)}, bf16[1024,768]{1,0:T(8,128)(2,1)}, u32[]{:S(2)}, u32[]{:S(2)}) collective-permute-start(bf16[1024,768]{1,0:T(8,128)(2,1)} %maximum_select_fusion.1), channel_id=1, source_target_pairs={{0,2},{1,3},{2,0},{3,1},{4,6},{5,7},{6,4},{7,5},{8,10},{9,11},{10,... | collective-permute-start | bytes 4718600 | tf_op jit(solution)/shard_map/ppermute | solution.py:14
  399.3 9.0 %copy-start.60 = (bf16[768,512]{1,0:T(8,128)(2,1)S(1)}, bf16[768,512]{1,0:T(8,128)(2,1)}, u32[]{:S(2)}) copy-start(bf16[768,512]{1,0:T(8,128)(2,1)} %param.41) | copy-start | bytes 2359300
  414.0 130.0 %all-gather.8.cloned.1.call-start = ((), (), s32[]{:S(2)}) async-start(), calls=%async_computation.9 | async-start | bytes 3932160 | tf_op jit(solution)/shard_map/all_gather | solution.py:244
  480.4 66.7 %copy-start.35 = (pred[512,512]{0,1:T(8,128)(4,1)S(1)}, pred[512,512]{0,1:T(8,128)(4,1)}, u32[]{:S(2)}) copy-start(pred[512,512]{0,1:T(8,128)(4,1)} %copy-done.34) | copy-start | bytes 786436
  480.4 66.7 %copy-start.74 = (f32[3,512]{1,0:T(4,128)S(1)}, f32[3,512]{1,0:T(4,128)}, u32[]{:S(2)}) copy-start(f32[3,512]{1,0:T(4,128)} %copy-done.73) | copy-start | bytes 18436
  480.4 66.7 %copy-start.82 = (bf16[512]{0:T(512)(128)(2,1)S(1)}, bf16[512]{0:T(512)(128)(2,1)}, u32[]{:S(2)}) copy-start(bf16[512]{0:T(512)(128)(2,1)} %get-tuple-element.206) | copy-start | bytes 3076
  480.5 169.3 %reduce-scatter.11.cloned.1.call-start = ((), (), s32[]{:S(2)}) async-start(), calls=%async_computation.10 | async-start | bytes 3932160 | tf_op jit(solution)/shard_map/reduce_scatter | solution.py:260
  584.7 177.7 %all-reduce.8.cloned.1.call-start = ((), (), s32[]{:S(2)}) async-start(), calls=%async_computation.11 | async-start | bytes 14155776 | tf_op jit(solution)/shard_map/psum | solution.py:271
  607.1 42.7 %copy-start.31 = (bf16[512,768]{1,0:T(8,128)(2,1)S(1)}, bf16[512,768]{1,0:T(8,128)(2,1)}, u32[]{:S(2)}) copy-start(bf16[512,768]{1,0:T(8,128)(2,1)} %reduce-scatter.9.cloned.1.call-done) | copy-start | bytes 2359300
  607.1 42.7 %copy-start.76 = (f32[512]{0:T(512)S(1)}, f32[512]{0:T(512)}, u32[]{:S(2)}) copy-start(f32[512]{0:T(512)} %copy-done.75) | copy-start | bytes 6148
  (74 other events, 206.6 us)
Sparse Core Ops, SparseCore 0:
  9.6 66.1 all-gather.3
  101.8 59.0 reduce-scatter.4
  165.4 63.3 all-gather.5
  242.0 59.0 reduce-scatter.6
  414.1 60.4 reduce-scatter.8
  480.5 63.3 all-gather.7
  584.8 59.9 reduce-scatter.10
  649.7 112.7 all-reduce.7
